TPU v7x, 8 devices: a whole 2x2x1 slice. The times are simulated.
8 devices in a mesh: dp: 2 (over y, z), ep: 4 (over x, core).
Axes of the slice: x: 2, y: 2, z: 1, core: 2. Of those that a mesh axis runs over, the one named last changes fastest.
Arguments:
- x: bfloat16 [2, 4, 512, 2048], P('dp', 'ep'), parts along dimension 0
- expert: int32 [2, 4, 512, 8], P('dp', 'ep'), parts along dimension 0
- slot: int32 [2, 4, 512, 8], P('dp', 'ep'), parts along dimension 0
- gate: float32 [2, 4, 512, 8], P('dp', 'ep'), parts along dimension 0
- w_gate: bfloat16 [64, 2048, 1024], P('ep')
- w_up: bfloat16 [64, 2048, 1024], P('ep')
- w_down: bfloat16 [64, 1024, 2048], P('ep')
Outputs:
- y: bfloat16 [2, 4, 512, 2048], P('dp', 'ep'), parts along dimension 0
There are 2 independent parts. A program takes and returns all parts, laid end to end along the dimension named above; an argument that names none is the same for every part.
All inputs are finite; a program needn't handle non-finite values.
Results may differ from a plain program's by a relative error of at most 0.009.
Values are sent between devices in bfloat16 or wider.
A program may use at most 2 GiB of HBM per device.

v0:
```python
import jax
import jax.numpy as jnp
from jax import lax
from jax.sharding import NamedSharding, PartitionSpec as P


def einsum(form, a, b):
    return jnp.einsum(form, a.astype(jnp.float32), b.astype(jnp.float32))


def solution(mesh):
    def placed(v, *spec):
        return lax.with_sharding_constraint(v, NamedSharding(mesh, P(*spec)))

    def step(x, expert, slot, gate, w_gate, w_up, w_down):
        experts, (tokens, top) = w_gate.shape[0], expert.shape[2:]
        slots = 5 * tokens * top // (4 * experts)
        to_expert = jax.nn.one_hot(expert, experts, dtype=jnp.bfloat16)
        to_slot = jax.nn.one_hot(slot, slots, dtype=jnp.bfloat16)
        weighted = to_expert * gate[..., None].astype(jnp.bfloat16)
        dispatch = einsum("abtke,abtkc->abtec", to_expert, to_slot).astype(jnp.bfloat16)
        combine = einsum("abtke,abtkc->abtec", weighted, to_slot).astype(jnp.bfloat16)
        z = einsum("abtec,abtd->aebcd", dispatch, x).astype(jnp.bfloat16)
        z = placed(z, "dp", None, "ep", None, None)
        z = placed(z, "dp", "ep", None, None, None)
        h = jax.nn.silu(einsum("aebcd,edf->aebcf", z, w_gate))
        h = (h * einsum("aebcd,edf->aebcf", z, w_up)).astype(jnp.bfloat16)
        out = einsum("aebcf,efd->aebcd", h, w_down).astype(jnp.bfloat16)
        out = placed(out, "dp", "ep", None, None, None)
        out = placed(out, "dp", None, "ep", None, None)
        y = einsum("abtec,aebcd->abtd", combine, out)
        return y.astype(jnp.bfloat16)

    return step
```

profile of v0, /device:TPU:0, one launch (start us, length us, event | category | flops | bytes accessed | tf_op | source)
XLA Modules:
  0.0 739.8 jit_solution(974598615049914595)
XLA Ops:
  0.0 0.0 copy-start
  0.0 1.0 copy.11
  1.0 0.0 copy-start.2
  1.0 0.9 copy.9
  1.9 0.0 copy-start.4
  1.9 8.1 %convolution_convert_fusion.1 = bf16[512,64,80]{2,1,0:T(8,128)(2,1)} fusion(s32[512,8]{1,0:T(8,128)S(1)} %copy.11, s32[512,8]{1,0:T(8,128)S(1)} %copy.9), kind=kOutput, calls=%fused_computation.23 | convolution fusion | flops 45154304 | bytes 5275648 | tf_op jit(solution)/abtke,abtkc->abtec/dot_general | solution.py:8
  10.0 0.0 copy-done
  10.0 79.9 %convolution_convert_fusion = bf16[64,80,2048]{2,1,0:T(8,128)(2,1)} fusion(bf16[512,64,80]{2,1,0:T(8,128)(2,1)} %convolution_convert_fusion.1, bf16[1,1,512,2048]{3,2,1,0:T(8,128)(2,1)S(1)} %copy-done), kind=kOutput, calls=%fused_computation.18 | convolution fusion | flops 10747904000 | bytes 28311552 | tf_op jit(solution)/abtec,abtd->aebcd/dot_general | solution.py:8
  90.0 0.0 copy-done.2
  90.0 0.0 copy-done.4
  90.0 241.5 %all-to-all.4 = bf16[1,4,16,1,80,2048]{5,4,2,3,0,1:T(8,128)(2,1)} all-to-all(bf16[1,4,16,1,80,2048]{5,4,2,3,0,1:T(8,128)(2,1)} %bitcast.84), channel_id=1, replica_groups=mesh['dp'=2,'ep'=4] {'ep'}, dimensions={1} | all-to-all | bytes 41943040 | tf_op jit(solution)/sharding_constraint;jit(solution)/sharding_constraint | solution.py:13
  331.5 41.3 %fusion.2 = f32[16,4,80,1024]{3,2,1,0:T(8,128)} fusion(bf16[16,2048,1024]{2,1,0:T(8,128)(2,1)} %param.5, bf16[1,4,16,1,80,2048]{5,4,2,3,0,1:T(8,128)(2,1)} %all-to-all.4), kind=kOutput, calls=%fused_computation.2 | convolution fusion | flops 21474836480 | bytes 109051904 | tf_op jit(solution)/aebcd,edf->aebcf/dot_general | solution.py:8
  372.8 42.4 %fusion.6 = bf16[1,16,4,80,1024]{4,3,2,1,0:T(8,128)(2,1)} fusion(f32[16,4,80,1024]{3,2,1,0:T(8,128)} %fusion.2, bf16[16,2048,1024]{2,1,0:T(8,128)(2,1)} %param.4, bf16[1,4,16,1,80,2048]{5,4,2,3,0,1:T(8,128)(2,1)} %all-to-all.4), kind=kOutput, calls=%fused_computation.7 | convolution fusion | flops 21506293760 | bytes 119537664 | tf_op jit(solution)/aebcd,edf->aebcf/dot_general | solution.py:8
  415.3 38.2 %convert_bitcast_fusion = bf16[1,16,4,1,80,2048]{5,4,2,1,3,0:T(8,128)(2,1)} fusion(bf16[16,1024,2048]{2,1,0:T(8,128)(2,1)} %param.6, bf16[1,16,4,80,1024]{4,3,2,1,0:T(8,128)(2,1)} %fusion.6), kind=kOutput, calls=%fused_computation.15 | convolution fusion | flops 21485322240 | bytes 98566144 | tf_op jit(solution)/aebcf,efd->aebcd/dot_general | solution.py:8
  453.5 17.6 %copy.15 = bf16[1,16,4,1,80,2048]{5,4,1,3,0,2:T(8,128)(2,1)} copy(bf16[1,16,4,1,80,2048]{5,4,2,1,3,0:T(8,128)(2,1)} %convert_bitcast_fusion) | data formatting | bytes 41943040 | tf_op jit(solution)/sharding_constraint;jit(solution)/sharding_constraint | solution.py:13
  471.1 0.0 copy-start.6
  471.1 0.0 copy-start.3
  471.1 0.0 copy-start.5
  471.1 7.9 %all-to-all-start.1 = ((bf16[1,16,4,1,80,2048]{5,4,1,3,0,2:T(8,128)(2,1)}), bf16[1,16,4,1,80,2048]{5,4,1,3,0,2:T(8,128)(2,1)}, u32[]{:S(2)}, u32[]{:S(2)}) async-start(bf16[1,16,4,1,80,2048]{5,4,1,3,0,2:T(8,128)(2,1)} %copy.15), calls=%async_computation.1 | async-start | bytes 41943040 | tf_op jit(solution)/sharding_constraint;jit(solution)/sharding_constraint | solution.py:13
  479.0 0.0 copy-done.6
  479.0 0.2 copy.10
  479.2 0.0 copy-done.3
  479.2 0.0 copy-done.5
  479.2 8.8 %convolution_convert_fusion.2 = bf16[512,64,80]{2,1,0:T(8,128)(2,1)} fusion(s32[512,8]{1,0:T(8,128)S(1)} %copy-done.3, s32[512,8]{1,0:T(8,128)S(1)} %copy-done.5, bf16[512,8]{1,0:T(8,128)(2,1)S(1)} %copy.10), kind=kOutput, calls=%fused_computation.24 | convolution fusion | flops 45416448 | bytes 5283840 | tf_op jit(solution)/abtke,abtkc->abtec/dot_general | solution.py:8
  488.0 218.6 %all-to-all-done.1 = bf16[1,16,4,1,80,2048]{5,4,1,3,0,2:T(8,128)(2,1)} async-done(((bf16[1,16,4,1,80,2048]{5,4,1,3,0,2:T(8,128)(2,1)}), bf16[1,16,4,1,80,2048]{5,4,1,3,0,2:T(8,128)(2,1)}, u32[]{:S(2)}, u32[]{:S(2)}) %all-to-all-start.1) | async-done | bytes 20971552 | tf_op jit(solution)/sharding_constraint;jit(solution)/sharding_constraint | solution.py:13
  706.6 0.0 copy-start.1
  706.6 32.9 %fusion.26 = bf16[1,1,512,2048]{3,2,1,0:T(8,128)(2,1)} fusion(bf16[64,80,2048]{2,1,0:T(8,128)(2,1)} %bitcast.25, bf16[512,64,80]{2,1,0:T(8,128)(2,1)} %convolution_convert_fusion.2), kind=kOutput, calls=%fused_computation.26 | convolution fusion | flops 10738466816 | bytes 28311552 | tf_op jit(solution)/abtec,aebcd->abtd/dot_general | solution.py:8
  739.6 0.0 copy-done.1
  (1 shorter events, 0.0 us)
Async XLA Ops:
  0.0 10.0 %copy-start = (bf16[1,1,512,2048]{3,2,1,0:T(8,128)(2,1)S(1)}, bf16[1,1,512,2048]{3,2,1,0:T(8,128)(2,1)}, u32[]{:S(2)}) copy-start(bf16[1,1,512,2048]{3,2,1,0:T(8,128)(2,1)} %param.3) | copy-start | bytes 6291460
  1.0 89.0 %copy-start.2 = (s32[512,8]{1,0:T(8,128)}, s32[512,8]{1,0:T(8,128)S(1)}, u32[]{:S(2)}) copy-start(s32[512,8]{1,0:T(8,128)S(1)} %copy.11) | copy-start | bytes 49156
  1.9 88.1 %copy-start.4 = (s32[512,8]{1,0:T(8,128)}, s32[512,8]{1,0:T(8,128)S(1)}, u32[]{:S(2)}) copy-start(s32[512,8]{1,0:T(8,128)S(1)} %copy.9) | copy-start | bytes 49156
  471.1 7.9 %copy-start.6 = (f32[1,1,512,8]{2,3,1,0:T(8,128)S(1)}, f32[1,1,512,8]{2,3,1,0:T(8,128)}, u32[]{:S(2)}) copy-start(f32[1,1,512,8]{2,3,1,0:T(8,128)} %param.1) | copy-start | bytes 49156
  471.1 8.1 %copy-start.3 = (s32[512,8]{1,0:T(8,128)S(1)}, s32[512,8]{1,0:T(8,128)}, u32[]{:S(2)}) copy-start(s32[512,8]{1,0:T(8,128)} %copy-done.2) | copy-start | bytes 49156
  471.1 8.1 %copy-start.5 = (s32[512,8]{1,0:T(8,128)S(1)}, s32[512,8]{1,0:T(8,128)}, u32[]{:S(2)}) copy-start(s32[512,8]{1,0:T(8,128)} %copy-done.4) | copy-start | bytes 49156
  471.1 235.5 %all-to-all-start.1 = ((bf16[1,16,4,1,80,2048]{5,4,1,3,0,2:T(8,128)(2,1)}), bf16[1,16,4,1,80,2048]{5,4,1,3,0,2:T(8,128)(2,1)}, u32[]{:S(2)}, u32[]{:S(2)}) async-start(bf16[1,16,4,1,80,2048]{5,4,1,3,0,2:T(8,128)(2,1)} %copy.15), calls=%async_computation.1 | async-start | bytes 41943040 | tf_op jit(solution)/sharding_constraint;jit(solution)/sharding_constraint | solution.py:13
  706.6 32.9 %copy-start.1 = (bf16[1,1,512,2048]{3,2,1,0:T(8,128)(2,1)S(1)}, bf16[1,1,512,2048]{3,2,1,0:T(8,128)(2,1)}, u32[]{:S(2)}) copy-start(bf16[1,1,512,2048]{3,2,1,0:T(8,128)(2,1)} %param.3) | copy-start | bytes 6291460
where the time goes:
time: 743 us; the launch traced here: 740 us
  matrix products  252 us (34%)
  blocking collectives  242 us (33%)
  waiting for transfers between devices  219 us (29%)
  local copies, waits for them, and re-layouts  19.6 us (3%)
  starting transfers between devices  7.87 us (1%)
    dot_general x7, matrix products, einsum(): return jnp.einsum(form, a.astype(jnp.float32), b.astype(jnp.float32))  252 us
    another operation x1, blocking collectives, placed(): return lax.with_sharding_constraint(v, NamedSharding(mesh, P(*spec)))  242 us
    another operation x1, waiting for transfers between devices, placed(): return lax.with_sharding_constraint(v, NamedSharding(mesh, P(*spec)))  219 us
    another operation x1, local copies, waits for them, and re-layouts, placed(): return lax.with_sharding_constraint(v, NamedSharding(mesh, P(*spec)))  17.6 us
  transfers between devices with their start and end apart: 1, of which 1 were waited for; matrix products, arithmetic and copies ran while one was open for 1% of the time, Pallas kernels for 0%

commit v1 on v0

v1 whole, which is shorter than its diff:
```python
import functools

import jax
import jax.numpy as jnp
from jax import lax
from jax.experimental import pallas as pl
from jax.experimental.pallas import tpu as pltpu
from jax.sharding import PartitionSpec as P


F32, BF16 = jnp.float32, jnp.bfloat16


def slots_of(expert, slot, e):
    return jnp.max(jnp.where(expert == e, slot, -1), axis=0, keepdims=True)


def gates_of(expert, gate, e):
    return jnp.sum(jnp.where(expert == e, gate, 0.0), axis=0, keepdims=True)


def up_kernel(parts, cap, fblk, e_ref, s_ref, *refs):
    n = sum(len(p) for p in parts)
    xs, (wg_ref, wu_ref, h_ref, z_ref) = refs[:n], refs[n:]
    e = pl.program_id(0)
    rows = lax.broadcasted_iota(jnp.int32, (cap, e_ref.shape[2]), 0)
    k = 0
    for i, part in enumerate(parts):
        sl = slots_of(e_ref[i], s_ref[i], e)
        pick = jnp.where(rows == sl, 1.0, 0.0).astype(BF16)
        z, at = None, 0
        for tokens in part:
            d = jnp.dot(pick[:, at : at + tokens], xs[k][...], preferred_element_type=F32)
            z, at, k = d if z is None else z + d, at + tokens, k + 1
        z_ref[pl.ds(i * cap, cap), :] = z.astype(BF16)
    for f in range(0, wg_ref.shape[2], fblk):
        g = jnp.dot(z_ref[...], wg_ref[0, :, f : f + fblk], preferred_element_type=F32)
        u = jnp.dot(z_ref[...], wu_ref[0, :, f : f + fblk], preferred_element_type=F32)
        h_ref[0, :, f : f + fblk] = (g * jax.nn.sigmoid(g) * u).astype(BF16)


def up(expert, slot, xs, parts, w_gate, w_up, cap, fblk=256):
    n_e, d, ff = w_gate.shape
    s, _, tokens = expert.shape
    whole = lambda a: pl.BlockSpec(a.shape, lambda e: (0,) * a.ndim, pipeline_mode=pl.Buffered(1))
    return pl.pallas_call(
        functools.partial(up_kernel, parts, cap, fblk),
        grid=(n_e,),
        out_shape=jax.ShapeDtypeStruct((n_e, s * cap, ff), BF16),
        in_specs=[whole(expert), whole(slot)]
        + [whole(x) for x in xs]
        + [pl.BlockSpec((1, d, ff), lambda e: (e, 0, 0))] * 2,
        out_specs=pl.BlockSpec((1, s * cap, ff), lambda e: (e, 0, 0)),
        scratch_shapes=[pltpu.VMEM((s * cap, d), BF16)],
        cost_estimate=pl.CostEstimate(
            flops=n_e * s * cap * d * (4 * ff + 2 * tokens),
            bytes_accessed=4 * n_e * d * ff,
            transcendentals=n_e * s * cap * ff,
        ),
    )(expert, slot, *xs, w_gate, w_up)


def down_kernel(cap, eb, e_ref, s_ref, g_ref, h_ref, w_ref, o0_ref, o1_ref, out_ref, c_ref):
    step = pl.program_id(0)
    outs = (o0_ref, o1_ref)
    rows = lax.broadcasted_iota(jnp.int32, (cap, e_ref.shape[2]), 0)
    for b in range(eb):
        e = step * eb + b
        at = pl.multiple_of(e * cap, cap)
        o = jnp.dot(h_ref[e], w_ref[b], preferred_element_type=F32).astype(BF16)
        for i in range(len(outs)):
            sl = slots_of(e_ref[i], s_ref[i], e)
            ga = gates_of(e_ref[i], g_ref[i], e)
            c_ref[i, pl.ds(at, cap), :] = jnp.where(rows == sl, ga, 0.0).astype(BF16)
            out_ref[i, pl.ds(at, cap), :] = o[i * cap : (i + 1) * cap]

    @pl.when(step == pl.num_programs(0) - 1)
    def _():
        for i, o_ref in enumerate(outs):
            for t in range(0, o_ref.shape[0], 256):
                y = lax.dot_general(
                    c_ref[i, :, t : t + 256], out_ref[i], (((0,), (0,)), ((), ())),
                    preferred_element_type=F32,
                )
                o_ref[t : t + 256, :] = y.astype(o_ref.dtype)


def down(expert, slot, gate, h, w_down, start, cols, cap, eb):
    n_e, ff, _ = w_down.shape
    s, _, tokens = expert.shape
    at = start // cols
    assert at * cols == start
    whole = lambda a: pl.BlockSpec(a.shape, lambda e: (0,) * a.ndim, pipeline_mode=pl.Buffered(1))
    out = pl.BlockSpec((tokens, cols), lambda e: (0, 0), pipeline_mode=pl.Buffered(1))
    return pl.pallas_call(
        functools.partial(down_kernel, cap, eb),
        grid=(n_e // eb,),
        out_shape=[
            jax.ShapeDtypeStruct((tokens, cols), F32),
            jax.ShapeDtypeStruct((tokens, cols), BF16),
        ],
        in_specs=[whole(expert), whole(slot), whole(gate), whole(h),
                  pl.BlockSpec((eb, ff, cols), lambda e: (e, 0, at))],
        out_specs=[out, out],
        scratch_shapes=[
            pltpu.VMEM((s, n_e * cap, cols), BF16),
            pltpu.VMEM((s, n_e * cap, tokens), BF16),
        ],
        cost_estimate=pl.CostEstimate(
            flops=2 * n_e * s * cap * cols * (ff + tokens),
            bytes_accessed=2 * n_e * cols * ff,
            transcendentals=0,
        ),
    )(expert, slot, gate, h, w_down)


def solution(mesh):
    members = mesh.shape["ep"]

    def local(x, expert, slot, gate, w_gate, w_up, w_down):
        x = x[0, 0]
        tokens, d = x.shape
        top = expert.shape[-1]
        n_e = w_gate.shape[0]
        cap = 5 * tokens * top // (4 * n_e * members)
        me = lax.axis_index("ep")

        def cross(v):
            return lax.ppermute(v, "ep", [(i, i ^ 2) for i in range(members)])

        def sibling(v):
            return lax.ppermute(v, "ep", [(i, i ^ 1) for i in range(members)])

        meta = jnp.concatenate(
            [expert[0, 0].T.astype(F32), jnp.minimum(slot[0, 0], cap).T.astype(F32),
             gate[0, 0].T.astype(BF16).astype(F32)], axis=0)
        cross_x = [cross(x[: tokens // 2]), cross(x[tokens // 2 :])]
        sib_x = sibling(x)
        metas = lax.all_gather(meta, "ep")

        def routing(sources):
            m = jnp.stack([lax.dynamic_index_in_dim(metas, i, keepdims=False) for i in sources])
            return (m[:, :top].astype(jnp.int32) - me * n_e, m[:, top : 2 * top].astype(jnp.int32),
                    m[:, 2 * top :])

        le, ls, lg = routing([me, me ^ 1])
        re, rs, rg = routing([me ^ 2, me ^ 3])

        h_l = up(le, ls, [x, sib_x], [[tokens], [tokens]], w_gate, w_up, cap)
        cross_x, h_l = lax.optimization_barrier((cross_x, h_l))
        fwd_x = [sibling(v) for v in cross_x]
        half = [v.shape[0] for v in cross_x]
        h_r = up(re, rs, cross_x + fwd_x, [half, half], w_gate, w_up, cap)

        both, back = [], []
        for n, (start, cols) in enumerate(((0, 256), (256, 256), (512, 512), (1024, 1024))):
            mine, other = down(re, rs, rg, h_r, w_down, start, cols, cap, 2048 // cols)
            if n:
                mine, other, both[-1] = lax.optimization_barrier((mine, other, both[-1]))
                back.append(cross(both[-1]))
            both.append((mine + sibling(other).astype(F32)).astype(BF16))
            h_r, _ = lax.optimization_barrier((h_r, mine))
        h_l, _ = lax.optimization_barrier((h_l, mine))
        own0, other0 = down(le, ls, lg, h_l, w_down, 0, d // 2, cap, 2)
        own0, other0, both[-1] = lax.optimization_barrier((own0, other0, both[-1]))
        back.append(cross(both[-1]))
        h_l, _ = lax.optimization_barrier((h_l, own0))
        own1, other1 = down(le, ls, lg, h_l, w_down, d // 2, d // 2, cap, 2)
        other = jnp.concatenate([sibling(other0), sibling(other1)], axis=1)
        y = jnp.concatenate([own0, own1], axis=1) + other.astype(F32) + jnp.concatenate(back, axis=1).astype(F32)
        return y.astype(BF16)[None, None]

    tok = P("dp", "ep", None, None)
    w = P("ep", None, None)

    return jax.shard_map(local, mesh=mesh, in_specs=(tok,) * 4 + (w,) * 3, out_specs=tok, check_vma=False)
```

time: 743 us -> 318 us (0.43)
  matrix products: 252 us -> 0 us
  Pallas kernels: 0 us -> 197 us
  blocking collectives: 242 us -> 50.8 us
  waiting for transfers between devices: 219 us -> 47.8 us
  local copies, waits for them, and re-layouts: 19.6 us -> 5.45 us
  other arithmetic: 0.01 us -> 8.98 us
    dot_general x7 -> x0, matrix products: 252 us -> none  [einsum(): return jnp.einsum(form, a.astype(jnp.float32), b.astype(jnp.float32))]
    another operation x1 -> x0, blocking collectives: 242 us -> none  [placed(): return lax.with_sharding_constraint(v, NamedSharding(mesh, P(*spec)))]
    another operation x1 -> x0, waiting for transfers between devices: 219 us -> none  [placed(): return lax.with_sharding_constraint(v, NamedSharding(mesh, P(*spec)))]
    pallas_call x0 -> x8, Pallas kernels: none -> 197 us  [the longest x2 104 us: up(): pl.pallas_call(functools.partial(up_kernel, parts, cap, fblk), grid=(n_e,...]
    all_gather x0 -> x1, blocking collectives: none -> 50.8 us  [local(): metas = lax.all_gather(meta, 'ep')]
    ppermute x0 -> x15, waiting for transfers between devices: none -> 47.8 us  [the longest x6 45.4 us: cross(): return lax.ppermute(v, 'ep', [(i, i ^ 2) for i in range(members)])]
    another operation x1 -> x0, local copies, waits for them, and re-layouts: 17.6 us -> none  [placed(): return lax.with_sharding_constraint(v, NamedSharding(mesh, P(*spec)))]
    another operation x1 -> x0, starting transfers between devices: 7.87 us -> none  [placed(): return lax.with_sharding_constraint(v, NamedSharding(mesh, P(*spec)))]
  transfers between devices with their start and end apart: 1 -> 15, of which waited for: 1 -> 4; matrix products, arithmetic and copies ran while one was open for 1% -> 2% of each run, Pallas kernels for 0% -> 36%
where the time goes in v1:
time: 318 us; the launch traced here: 317 us
  Pallas kernels  197 us (62%)
  blocking collectives  50.8 us (16%)
  waiting for transfers between devices  47.8 us (15%)
  other arithmetic  8.98 us (3%)
  starting transfers between devices  7.79 us (2%)
  local copies, waits for them, and re-layouts  5.45 us (2%)
    pallas_call x2, Pallas kernels, up(): pl.pallas_call(functools.partial(up_kernel, parts, cap, fblk), grid=(n_e,...  104 us
    pallas_call x6, Pallas kernels, down(): pl.pallas_call(functools.partial(down_kernel, cap, eb), grid=(n_e // eb,)...  92.3 us
    all_gather x1, blocking collectives, local(): metas = lax.all_gather(meta, 'ep')  50.8 us
    ppermute x6, waiting for transfers between devices, cross(): return lax.ppermute(v, 'ep', [(i, i ^ 2) for i in range(members)])  45.4 us
  transfers between devices with their start and end apart: 15, of which 4 were waited for; matrix products, arithmetic and copies ran while one was open for 2% of the time, Pallas kernels for 36%

profile of v1, /device:TPU:0, one launch (start us, length us, event | category | flops | bytes accessed | tf_op | source)
XLA Modules:
  0.0 317.5 jit_solution(4231716528864105395)
XLA Ops:
  0.0 0.9 collective-permute-start.2
  0.9 3.1 slice_bitcast_fusion
  4.0 2.5 collective-permute-start
  6.5 0.0 collective-permute-start.1
  6.5 50.8 %all-gather = f32[96,512]{1,0:T(8,128)S(1)} all-gather(f32[24,512]{1,0:T(8,128)S(1)} %pad_maximum_fusion), channel_id=2, replica_groups=mesh['dp'=2,'ep'=4] {'ep'}, dimensions={0}, use_global_device_ids=true | all-gather | bytes 245760 | tf_op jit(solution)/shard_map/all_gather | solution.py:139
  57.3 0.6 fusion.11.e_ref
  57.9 0.6 pad_maximum_fusion.2
  58.6 0.0 collective-permute-done.2.refs_1_
  58.6 1.3 copy-done
  59.9 52.2 %shard_map.73.h_ref = bf16[16,160,1024]{2,1,0:T(8,128)(2,1)} custom-call(s32[2,8,512]{2,1,0:T(8,128)} %fusion.11.e_ref, s32[2,8,512]{2,1,0:T(8,128)} %get-tuple-element.78.s_ref, bf16[512,2048]{1,0:T(8,128)(2,1)} %bitcast.28, bf16[512,2048]{1,0:T(8,128)(2,1)} %copy-done, bf16[16,2048,1024]{2,1,0:T(8,128)(2,1)} %refs_4_.1, bf16[16,2048,1024]{2,1,0:T(8,128)(2,1)} %refs_5_.1), custom_call_target="tpu_custom_call" | custom-call | flops 26843545600 | bytes 134217728 | tf_op jit(solution)/shard_map/pallas_call | solution.py:46
  112.1 0.0 collective-permute-done.refs_0_
  112.1 0.0 collective-permute-done.1.refs_1_
  112.1 0.0 collective-permute-start.3
  112.1 0.5 collective-permute-start.4
  112.6 0.6 fusion.6.e_ref
  113.2 0.6 pad_maximum_fusion.1
  113.9 0.9 collective-permute-done.3.refs_2_
  114.8 1.5 collective-permute-done.4.refs_3_
  116.3 1.0 copy-done.5
  117.2 52.1 %shard_map.74.h_ref = bf16[16,160,1024]{2,1,0:T(8,128)(2,1)} custom-call(s32[2,8,512]{2,1,0:T(8,128)} %fusion.6.e_ref, s32[2,8,512]{2,1,0:T(8,128)} %get-tuple-element.76.s_ref, bf16[256,2048]{1,0:T(8,128)(2,1)} %copy-done.3, bf16[256,2048]{1,0:T(8,128)(2,1)} %collective-permute-done.1.refs_1_, bf16[256,2048]{1,0:T(8,128)(2,1)} %copy-done.4, ...), custom_call_target="tpu_custom_call" | custom-call | flops 26843545600 | bytes 134217728 | tf_op jit(solution)/shard_map/pallas_call | solution.py:46
  169.4 8.5 %shard_map.75 = (f32[512,256]{1,0:T(8,128)}, bf16[512,256]{1,0:T(8,128)(2,1)}) custom-call(s32[2,8,512]{2,1,0:T(8,128)} %fusion.6.e_ref, s32[2,8,512]{2,1,0:T(8,128)} %get-tuple-element.76.s_ref, f32[2,8,512]{2,1,0:T(8,128)} %get-tuple-element.75.g_ref, bf16[16,160,1024]{2,1,0:T(8,128)(2,1)} %shard_map.74.h_ref, bf16[16,1024,2048]{2,1,0:T(8,128)(2,1)} %w_ref.11), custom_call_target="tpu_custom_call" | custom-call | flops 2013265920 | bytes 8388608 | tf_op jit(solution)/shard_map/pallas_call | solution.py:95
  177.9 0.1 collective-permute-start.5
  178.0 8.5 %shard_map.76 = (f32[512,256]{1,0:T(8,128)}, bf16[512,256]{1,0:T(8,128)(2,1)}) custom-call(s32[2,8,512]{2,1,0:T(8,128)} %fusion.6.e_ref, s32[2,8,512]{2,1,0:T(8,128)} %get-tuple-element.76.s_ref, f32[2,8,512]{2,1,0:T(8,128)} %get-tuple-element.75.g_ref, bf16[16,160,1024]{2,1,0:T(8,128)(2,1)} %shard_map.74.h_ref, bf16[16,1024,2048]{2,1,0:T(8,128)(2,1)} %w_ref.11), custom_call_target="tpu_custom_call" | custom-call | flops 2013265920 | bytes 8388608 | tf_op jit(solution)/shard_map/pallas_call | solution.py:95
  186.5 0.0 collective-permute-done.5
  186.5 0.1 add_convert_fusion.3
  186.6 0.4 collective-permute-start.6
  187.0 12.3 %shard_map.77 = (f32[512,512]{1,0:T(8,128)}, bf16[512,512]{1,0:T(8,128)(2,1)}) custom-call(s32[2,8,512]{2,1,0:T(8,128)} %fusion.6.e_ref, s32[2,8,512]{2,1,0:T(8,128)} %get-tuple-element.76.s_ref, f32[2,8,512]{2,1,0:T(8,128)} %get-tuple-element.75.g_ref, bf16[16,160,1024]{2,1,0:T(8,128)(2,1)} %shard_map.74.h_ref, bf16[16,1024,2048]{2,1,0:T(8,128)(2,1)} %w_ref.11), custom_call_target="tpu_custom_call" | custom-call | flops 4026531840 | bytes 16777216 | tf_op jit(solution)/shard_map/pallas_call | solution.py:95
  199.3 0.0 collective-permute-done.6
  199.4 0.8 add_convert_fusion.2
  200.1 0.1 collective-permute-start.7
  200.3 21.0 %shard_map.78 = (f32[512,1024]{1,0:T(8,128)}, bf16[512,1024]{1,0:T(8,128)(2,1)}) custom-call(s32[2,8,512]{2,1,0:T(8,128)} %fusion.6.e_ref, s32[2,8,512]{2,1,0:T(8,128)} %get-tuple-element.76.s_ref, f32[2,8,512]{2,1,0:T(8,128)} %get-tuple-element.75.g_ref, bf16[16,160,1024]{2,1,0:T(8,128)(2,1)} %shard_map.74.h_ref, bf16[16,1024,2048]{2,1,0:T(8,128)(2,1)} %w_ref.11), custom_call_target="tpu_custom_call" | custom-call | flops 8053063680 | bytes 33554432 | tf_op jit(solution)/shard_map/pallas_call | solution.py:95
  221.3 0.9 add_convert_fusion.1
  222.2 0.2 collective-permute-start.8
  222.5 21.0 %shard_map.79 = (f32[512,1024]{1,0:T(8,128)}, bf16[512,1024]{1,0:T(8,128)(2,1)}) custom-call(s32[2,8,512]{2,1,0:T(8,128)} %fusion.11.e_ref, s32[2,8,512]{2,1,0:T(8,128)} %get-tuple-element.78.s_ref, f32[2,8,512]{2,1,0:T(8,128)} %get-tuple-element.77.g_ref, bf16[16,160,1024]{2,1,0:T(8,128)(2,1)} %shard_map.73.h_ref, bf16[16,1024,2048]{2,1,0:T(8,128)(2,1)} %w_ref.11), custom_call_target="tpu_custom_call" | custom-call | flops 8053063680 | bytes 33554432 | tf_op jit(solution)/shard_map/pallas_call | solution.py:95
  243.5 1.6 add_convert_fusion
  245.1 0.0 copy-start.1
  245.1 20.9 %shard_map.80 = (f32[512,1024]{1,0:T(8,128)}, bf16[512,1024]{1,0:T(8,128)(2,1)}) custom-call(s32[2,8,512]{2,1,0:T(8,128)} %fusion.11.e_ref, s32[2,8,512]{2,1,0:T(8,128)} %get-tuple-element.78.s_ref, f32[2,8,512]{2,1,0:T(8,128)} %get-tuple-element.77.g_ref, bf16[16,160,1024]{2,1,0:T(8,128)(2,1)} %shard_map.73.h_ref, bf16[16,1024,2048]{2,1,0:T(8,128)(2,1)} %w_ref.11), custom_call_target="tpu_custom_call" | custom-call | flops 8053063680 | bytes 33554432 | tf_op jit(solution)/shard_map/pallas_call | solution.py:95
  266.0 0.3 collective-permute-start.10
  266.3 0.2 collective-permute-start.9
  266.5 0.2 collective-permute-start.14
  266.7 1.8 collective-permute-start.11
  268.5 0.2 collective-permute-start.13
  268.8 29.4 %collective-permute-done.11 = bf16[512,256]{1,0:T(8,128)(2,1)S(1)} collective-permute-done((bf16[512,256]{1,0:T(8,128)(2,1)S(1)}, bf16[512,256]{1,0:T(8,128)(2,1)S(1)}, u32[]{:S(2)}, u32[]{:S(2)}) %collective-permute-start.11) | collective-permute-done | bytes 262176 | tf_op jit(solution)/shard_map/ppermute | solution.py:129
  298.2 0.2 collective-permute-start.12
  298.4 15.9 %collective-permute-done.12 = bf16[512,256]{1,0:T(8,128)(2,1)S(1)} collective-permute-done((bf16[512,256]{1,0:T(8,128)(2,1)}, bf16[512,256]{1,0:T(8,128)(2,1)S(1)}, u32[]{:S(2)}, u32[]{:S(2)}) %collective-permute-start.12) | collective-permute-done | bytes 262176 | tf_op jit(solution)/shard_map/ppermute | solution.py:129
  314.3 0.0 collective-permute-done.13
  314.3 0.0 collective-permute-done.10
  314.4 3.1 fusion.1
  (29 shorter events, 0.1 us)
Async XLA Ops:
  0.0 6.5 %copy-start.9 = (f32[1,1,512,8]{2,3,1,0:T(8,128)S(1)}, f32[1,1,512,8]{2,3,1,0:T(8,128)}, u32[]{:S(2)}) copy-start(f32[1,1,512,8]{2,3,1,0:T(8,128)} %param.10) | copy-start | bytes 49156
  0.0 6.5 %copy-start.11 = (s32[1,1,512,8]{2,3,1,0:T(8,128)S(1)}, s32[1,1,512,8]{2,3,1,0:T(8,128)}, u32[]{:S(2)}) copy-start(s32[1,1,512,8]{2,3,1,0:T(8,128)} %param.8) | copy-start | bytes 49156
  0.0 6.5 %copy-start.10 = (s32[1,1,512,8]{2,3,1,0:T(8,128)S(1)}, s32[1,1,512,8]{2,3,1,0:T(8,128)}, u32[]{:S(2)}) copy-start(s32[1,1,512,8]{2,3,1,0:T(8,128)} %param.9) | copy-start | bytes 49156
  0.0 58.6 %collective-permute-start.2 = (bf16[512,2048]{1,0:T(8,128)(2,1)}, bf16[512,2048]{1,0:T(8,128)(2,1)S(1)}, u32[]{:S(2)}, u32[]{:S(2)}) collective-permute-start(bf16[512,2048]{1,0:T(8,128)(2,1)} %bitcast.27), channel_id=1, source_target_pairs={{0,1},{1,0},{2,3},{3,2},{4,5},{5,4},{6,7},{7,6}} | collective-permute-start | bytes 6291464 | tf_op jit(solution)/shard_map/ppermute | solution.py:132
  4.0 108.1 %collective-permute-start = (bf16[256,2048]{1,0:T(8,128)(2,1)}, bf16[256,2048]{1,0:T(8,128)(2,1)S(1)}, u32[]{:S(2)}, u32[]{:S(2)}) collective-permute-start(bf16[256,2048]{1,0:T(8,128)(2,1)} %get-tuple-element.70), channel_id=1, source_target_pairs={{0,2},{1,3},{2,0},{3,1},{4,6},{5,7},{6,4},{7,5}} | collective-permute-start | bytes 3145736 | tf_op jit(solution)/shard_map/ppermute | solution.py:129
  6.5 105.6 %collective-permute-start.1 = (bf16[256,2048]{1,0:T(8,128)(2,1)}, bf16[256,2048]{1,0:T(8,128)(2,1)}, u32[]{:S(2)}, u32[]{:S(2)}) collective-permute-start(bf16[256,2048]{1,0:T(8,128)(2,1)} %get-tuple-element.69), channel_id=1, source_target_pairs={{0,2},{1,3},{2,0},{3,1},{4,6},{5,7},{6,4},{7,5}} | collective-permute-start | bytes 3145736 | tf_op jit(solution)/shard_map/ppermute | solution.py:129
  58.6 1.3 copy-start
  112.1 4.2 %copy-start.3 = (bf16[256,2048]{1,0:T(8,128)(2,1)}, bf16[256,2048]{1,0:T(8,128)(2,1)S(1)}, u32[]{:S(2)}) copy-start(bf16[256,2048]{1,0:T(8,128)(2,1)S(1)} %collective-permute-done.refs_0_) | copy-start | bytes 3145732
  112.1 2.7 collective-permute-start.3
  112.1 4.1 %collective-permute-start.4 = (bf16[256,2048]{1,0:T(8,128)(2,1)}, bf16[256,2048]{1,0:T(8,128)(2,1)S(1)}, u32[]{:S(2)}, u32[]{:S(2)}) collective-permute-start(bf16[256,2048]{1,0:T(8,128)(2,1)} %collective-permute-done.1.refs_1_), channel_id=1, source_target_pairs={{0,1},{1,0},{2,3},{3,2},{4,5},{5,4},{6,7},{7,6}} | collective-permute-start | bytes 3145736 | tf_op jit(solution)/shard_map/ppermute | solution.py:132
  114.8 1.5 copy-start.4
  116.3 1.0 copy-start.5
  177.9 8.7 %collective-permute-start.5 = (bf16[512,256]{1,0:T(8,128)(2,1)}, bf16[512,256]{1,0:T(8,128)(2,1)S(1)}, u32[]{:S(2)}, u32[]{:S(2)}) collective-permute-start(bf16[512,256]{1,0:T(8,128)(2,1)} %get-tuple-element.44), channel_id=1, source_target_pairs={{0,1},{1,0},{2,3},{3,2},{4,5},{5,4},{6,7},{7,6}} | collective-permute-start | bytes 786440 | tf_op jit(solution)/shard_map/ppermute | solution.py:132
  178.0 8.5 %copy-start.8 = (f32[512,256]{1,0:T(8,128)S(1)}, f32[512,256]{1,0:T(8,128)}, u32[]{:S(2)}) copy-start(f32[512,256]{1,0:T(8,128)} %get-tuple-element.40) | copy-start | bytes 1572868
  186.6 12.8 %copy-start.7 = (f32[512,256]{1,0:T(8,128)S(1)}, f32[512,256]{1,0:T(8,128)}, u32[]{:S(2)}) copy-start(f32[512,256]{1,0:T(8,128)} %get-tuple-element.45) | copy-start | bytes 1572868
  186.6 12.7 %collective-permute-start.6 = (bf16[512,256]{1,0:T(8,128)(2,1)}, bf16[512,256]{1,0:T(8,128)(2,1)S(1)}, u32[]{:S(2)}, u32[]{:S(2)}) collective-permute-start(bf16[512,256]{1,0:T(8,128)(2,1)} %get-tuple-element.49), channel_id=1, source_target_pairs={{0,1},{1,0},{2,3},{3,2},{4,5},{5,4},{6,7},{7,6}} | collective-permute-start | bytes 786440 | tf_op jit(solution)/shard_map/ppermute | solution.py:132
  200.1 21.2 %copy-start.6 = (f32[512,512]{1,0:T(8,128)S(1)}, f32[512,512]{1,0:T(8,128)}, u32[]{:S(2)}) copy-start(f32[512,512]{1,0:T(8,128)} %get-tuple-element.50) | copy-start | bytes 3145732
  200.1 21.2 %collective-permute-start.7 = (bf16[512,512]{1,0:T(8,128)(2,1)}, bf16[512,512]{1,0:T(8,128)(2,1)S(1)}, u32[]{:S(2)}, u32[]{:S(2)}) collective-permute-start(bf16[512,512]{1,0:T(8,128)(2,1)} %get-tuple-element.54), channel_id=1, source_target_pairs={{0,1},{1,0},{2,3},{3,2},{4,5},{5,4},{6,7},{7,6}} | collective-permute-start | bytes 1572872 | tf_op jit(solution)/shard_map/ppermute | solution.py:132
  222.2 21.3 %collective-permute-start.8 = (bf16[512,1024]{1,0:T(8,128)(2,1)}, bf16[512,1024]{1,0:T(8,128)(2,1)}, u32[]{:S(2)}, u32[]{:S(2)}) collective-permute-start(bf16[512,1024]{1,0:T(8,128)(2,1)} %get-tuple-element.59), channel_id=1, source_target_pairs={{0,1},{1,0},{2,3},{3,2},{4,5},{5,4},{6,7},{7,6}} | collective-permute-start | bytes 3145736 | tf_op jit(solution)/shard_map/ppermute | solution.py:132
  222.5 21.0 %copy-start.2 = (f32[512,1024]{1,0:T(8,128)S(1)}, f32[512,1024]{1,0:T(8,128)}, u32[]{:S(2)}) copy-start(f32[512,1024]{1,0:T(8,128)} %get-tuple-element.55) | copy-start | bytes 6291460
  245.1 69.3 %copy-start.1 = (f32[512,1024]{1,0:T(8,128)S(1)}, f32[512,1024]{1,0:T(8,128)}, u32[]{:S(2)}) copy-start(f32[512,1024]{1,0:T(8,128)} %get-tuple-element.60) | copy-start | bytes 6291460
  266.0 48.3 %collective-permute-start.10 = (bf16[512,1024]{1,0:T(8,128)(2,1)}, bf16[512,1024]{1,0:T(8,128)(2,1)S(1)}, u32[]{:S(2)}, u32[]{:S(2)}) collective-permute-start(bf16[512,1024]{1,0:T(8,128)(2,1)} %get-tuple-element.64), channel_id=1, source_target_pairs={{0,1},{1,0},{2,3},{3,2},{4,5},{5,4},{6,7},{7,6}} | collective-permute-start | bytes 3145736 | tf_op jit(solution)/shard_map/ppermute | solution.py:132
  266.3 48.1 %collective-permute-start.9 = (bf16[512,1024]{1,0:T(8,128)(2,1)}, bf16[512,1024]{1,0:T(8,128)(2,1)S(1)}, u32[]{:S(2)}, u32[]{:S(2)}) collective-permute-start(bf16[512,1024]{1,0:T(8,128)(2,1)} %get-tuple-element.63), channel_id=1, source_target_pairs={{0,1},{1,0},{2,3},{3,2},{4,5},{5,4},{6,7},{7,6}} | collective-permute-start | bytes 3145736 | tf_op jit(solution)/shard_map/ppermute | solution.py:132
  266.5 47.8 %collective-permute-start.14 = (bf16[512,1024]{1,0:T(8,128)(2,1)S(1)}, bf16[512,1024]{1,0:T(8,128)(2,1)S(1)}, u32[]{:S(2)}, u32[]{:S(2)}) collective-permute-start(bf16[512,1024]{1,0:T(8,128)(2,1)S(1)} %add_convert_fusion), channel_id=1, source_target_pairs={{0,2},{1,3},{2,0},{3,1},{4,6},{5,7},{6,4},{7,5}} | collective-permute-start | bytes 3145736 | tf_op jit(solution)/shard_map/ppermute | solution.py:129
  266.7 31.4 %collective-permute-start.11 = (bf16[512,256]{1,0:T(8,128)(2,1)S(1)}, bf16[512,256]{1,0:T(8,128)(2,1)S(1)}, u32[]{:S(2)}, u32[]{:S(2)}) collective-permute-start(bf16[512,256]{1,0:T(8,128)(2,1)S(1)} %add_convert_fusion.3), channel_id=1, source_target_pairs={{0,2},{1,3},{2,0},{3,1},{4,6},{5,7},{6,4},{7,5}} | collective-permute-start | bytes 786440 | tf_op jit(solution)/shard_map/ppermute | solution.py:129
  268.5 45.8 %collective-permute-start.13 = (bf16[512,512]{1,0:T(8,128)(2,1)}, bf16[512,512]{1,0:T(8,128)(2,1)S(1)}, u32[]{:S(2)}, u32[]{:S(2)}) collective-permute-start(bf16[512,512]{1,0:T(8,128)(2,1)} %add_convert_fusion.1), channel_id=1, source_target_pairs={{0,2},{1,3},{2,0},{3,1},{4,6},{5,7},{6,4},{7,5}} | collective-permute-start | bytes 1572872 | tf_op jit(solution)/shard_map/ppermute | solution.py:129
  298.2 16.2 %collective-permute-start.12 = (bf16[512,256]{1,0:T(8,128)(2,1)}, bf16[512,256]{1,0:T(8,128)(2,1)S(1)}, u32[]{:S(2)}, u32[]{:S(2)}) collective-permute-start(bf16[512,256]{1,0:T(8,128)(2,1)} %add_convert_fusion.2), channel_id=1, source_target_pairs={{0,2},{1,3},{2,0},{3,1},{4,6},{5,7},{6,4},{7,5}} | collective-permute-start | bytes 786440 | tf_op jit(solution)/shard_map/ppermute | solution.py:129

commit v2 on v0

v2 whole, which is shorter than its diff:
```python
import functools

import jax
import jax.numpy as jnp
from jax import lax
from jax.experimental import pallas as pl
from jax.experimental.pallas import tpu as pltpu
from jax.sharding import PartitionSpec as P

F32, BF16 = jnp.float32, jnp.bfloat16
MESH = pl.DeviceIdType.MESH

EARLY = 6
RING, DRING = 8, 4
KC, CC, FB = 512, 512, 256


def moe_kernel(cap, meta_ref, x_ref, wg_ref, wu_ref, wd_ref, own_ref, sibr_ref, crossr_ref,
               metas, xs, wgr, wur, wdr, hl, hr, sibrecv, zr, zl,
               gsem, usem, dsem, xsem, msend, mrecv, xsend, xrecv,
               qsend_sem, qrecv_sem, csend_sem, crecv_sem, lsend_sem, lrecv_sem, osem):
    me = lax.axis_index("ep")
    sib = me + 1 - 2 * (me % 2)
    far = (me + 2) % 4
    peers = (sib, far, (sib + 2) % 4)
    n_e, d, ff = wg_ref.shape
    top, tokens = metas.shape[1] // 3, metas.shape[2]
    nk, nc = d // KC, d // CC
    first = me * n_e

    barrier = pltpu.get_barrier_semaphore()
    for p in peers:
        pl.semaphore_signal(barrier, inc=1, device_id={"ep": p}, device_id_type=MESH)

    late = n_e - EARLY
    phases = [("L", 0, 4 * EARLY)] + [("R", k, n_e) for k in range(nk)] + [("L", EARLY, 4 * late)]
    bases = [sum(p[2] for p in phases[:i]) for i in range(len(phases))]
    total = bases[-1] + phases[-1][2]

    def piece(pos, lo):
        def inside(i):
            kind, a, _ = phases[i]
            at = pos - bases[i]
            return (a + at // 4, at % 4) if kind == "L" else (at, a)
        e, k = inside(lo)
        if lo + 1 < len(phases):
            nxt = pos // bases[lo + 1]
            e1, k1 = inside(lo + 1)
            e, k = e + nxt * (e1 - e), k + nxt * (k1 - k)
        return e, k

    def fill(pos, e, k):
        slot = pos % RING
        rows = pl.ds(pl.multiple_of(k * KC, KC), KC)
        pltpu.make_async_copy(wg_ref.at[e, rows], wgr.at[slot], gsem.at[slot]).start()
        pltpu.make_async_copy(wu_ref.at[e, rows], wur.at[slot], usem.at[slot]).start()

    def filled(slot):
        pltpu.make_async_copy(wg_ref.at[0, pl.ds(0, KC)], wgr.at[slot], gsem.at[slot]).wait()
        pltpu.make_async_copy(wu_ref.at[0, pl.ds(0, KC)], wur.at[slot], usem.at[slot]).wait()

    def dfill(pos):
        slot, e, c = pos % DRING, pos % n_e, (pos // n_e) % nc
        cols = pl.ds(pl.multiple_of(c * CC, CC), CC)
        pltpu.make_async_copy(wd_ref.at[e, :, cols], wdr.at[slot], dsem.at[slot]).start()

    def dfilled(slot):
        pltpu.make_async_copy(wd_ref.at[0, :, pl.ds(0, CC)], wdr.at[slot], dsem.at[slot]).wait()

    def x_local(k):
        return pltpu.make_async_copy(x_ref.at[:, pl.ds(k * KC, KC)], xs.at[0, k], xsem.at[k])

    def x_copy(src, k):
        piece_ref = xs.at[2, k] if src == 3 else x_ref.at[:, pl.ds(k * KC, KC)]
        return pltpu.make_async_remote_copy(
            src_ref=piece_ref, dst_ref=xs.at[src, k], send_sem=xsend.at[src - 1, k],
            recv_sem=xrecv.at[src - 1, k], device_id={"ep": far if src == 2 else sib}, device_id_type=MESH)

    def meta_copy(src):
        return pltpu.make_async_remote_copy(
            src_ref=meta_ref, dst_ref=metas.at[src], send_sem=msend.at[src - 1],
            recv_sem=mrecv.at[src - 1], device_id={"ep": peers[src - 1]}, device_id_type=MESH)

    for k in range(nk):
        x_local(k).start()
    for pos in range(RING):
        fill(pos, pos // 4, pos % 4)
    metas[0] = meta_ref[...]
    pl.semaphore_wait(barrier, 3)
    for src in (1, 2, 3):
        meta_copy(src).start()
    for k in range(nk):
        x_copy(1, k).start()
    for k in range(nk):
        x_copy(2, k).start()

    slot_rows = lax.broadcasted_iota(jnp.int32, (cap, tokens), 0).astype(F32)

    def slots_of(src, e):
        hit = metas[src, 0:top, :] == (e + first).astype(F32)
        return jnp.max(jnp.where(hit, metas[src, top : 2 * top, :], -1.0), axis=0, keepdims=True)

    def gates_of(src, e):
        hit = metas[src, 0:top, :] == (e + first).astype(F32)
        return jnp.sum(jnp.where(hit, metas[src, 2 * top :, :], 0.0), axis=0, keepdims=True)

    def pick(src, e):
        return jnp.where(slot_rows == slots_of(src, e), 1.0, 0.0).astype(BF16)

    def dot(a, b):
        return jnp.dot(a, b, preferred_element_type=F32)

    def near(lo, count, after):
        _, e0, _ = phases[lo]

        def body(i, _):
            e = e0 + i
            for s in (0, 1):
                p = pick(s, e)
                for k in range(nk):
                    zl[s * cap : (s + 1) * cap, k * KC : (k + 1) * KC] = dot(p, xs[s, k]).astype(BF16)
            pos = bases[lo] + 4 * i
            at = pl.multiple_of(pos % RING, 4)
            for q in range(4):
                filled(at + q)
            for f in range(0, ff, FB):
                wg = wgr[pl.ds(at, 4), :, f : f + FB].reshape(d, FB)
                wu = wur[pl.ds(at, 4), :, f : f + FB].reshape(d, FB)
                g, u = dot(zl[...], wg), dot(zl[...], wu)
                hl[e, :, f : f + FB] = (g * jax.nn.sigmoid(g) * u).astype(BF16)

            def refill():
                for q in range(4):
                    nxt = pos + q + RING
                    fill(nxt, *piece(nxt, lo))

            if lo + 1 < len(phases):
                refill()
            else:
                pl.when(i < count - 2)(refill)
            after(i)
            return 0

        lax.fori_loop(0, count, body, 0)

    def pass_on(k):
        x_copy(2, k).wait_recv()
        x_copy(3, k).start()

    def far_phase(k, acc):
        lo = 1 + k
        x_copy(3, k).wait_recv()

        def body(i, _):
            if k + 1 < nk:
                @pl.when(i == n_e // 2 - 1)
                def _():
                    pass_on(k + 1)
            for b in (0, 1):
                for s in (0, 1):
                    zr[b, s * cap : (s + 1) * cap, :] = dot(pick(2 + s, 2 * i + b), xs[2 + s, k]).astype(BF16)
            for b in (0, 1):
                e = 2 * i + b
                pos = bases[lo] + e
                slot = pos % RING
                filled(slot)
                for f in range(0, ff, FB):
                    g = dot(zr[b], wgr[slot, :, f : f + FB])
                    u = dot(zr[b], wur[slot, :, f : f + FB])
                    if k:
                        g = g + acc[e, :, f : f + FB]
                        u = u + acc[e, :, ff + f : ff + f + FB]
                    if k == nk - 1:
                        hr[e, :, f : f + FB] = (g * jax.nn.sigmoid(g) * u).astype(BF16)
                    else:
                        acc[e, :, f : f + FB] = g
                        acc[e, :, ff + f : ff + f + FB] = u
                fill(pos + RING, *piece(pos + RING, lo))
            return 0

        lax.fori_loop(0, n_e // 2, body, 0)

    for k in range(nk):
        x_local(k).wait()
        x_copy(1, k).wait_recv()
    meta_copy(1).wait_recv()

    def first_pass_on(i):
        @pl.when(i == EARLY - 2)
        def _():
            pass_on(0)

    near(0, EARLY, first_pass_on)
    for pos in range(DRING):
        dfill(pos)
    meta_copy(2).wait_recv()
    meta_copy(3).wait_recv()

    def first_half(acc):
        for k in range(nk):
            far_phase(k, acc)

    pl.run_scoped(first_half, pltpu.VMEM((n_e, 2 * cap, 2 * ff), F32))

    def second_half(outs, cmat, yp, qsend, csend, lsend, yo):
        def cols(c):
            return pl.ds(pl.multiple_of(c * CC, CC), CC)

        def q_copy(c):
            return pltpu.make_async_remote_copy(
                src_ref=qsend.at[c], dst_ref=sibrecv.at[c], send_sem=qsend_sem.at[c],
                recv_sem=qrecv_sem.at[c], device_id={"ep": sib}, device_id_type=MESH)

        def c_copy(c):
            return pltpu.make_async_remote_copy(
                src_ref=csend.at[c], dst_ref=crossr_ref.at[:, cols(c)], send_sem=csend_sem.at[c],
                recv_sem=crecv_sem.at[c], device_id={"ep": far}, device_id_type=MESH)

        def l_copy(c):
            return pltpu.make_async_remote_copy(
                src_ref=lsend.at[c], dst_ref=sibr_ref.at[:, cols(c)], send_sem=lsend_sem.at[c],
                recv_sem=lrecv_sem.at[c], device_id={"ep": sib}, device_id_type=MESH)

        def o_copy(c):
            return pltpu.make_async_copy(yo.at[c], own_ref.at[:, cols(c)], osem.at[c])

        def cross_sum(c):
            q_copy(c).wait_recv()
            csend[c] = (yp[...] + sibrecv[c].astype(F32)).astype(BF16)
            c_copy(c).start()

        def combined(s, t):
            return lax.dot_general(cmat[s, :, t : t + 256], outs[s], (((0,), (0,)), ((), ())),
                                   preferred_element_type=F32)

        def down(side, h):
            def chunk(c, _):
                def body(i, _):
                    if side == 0:
                        @pl.when(i == 3)
                        def _():
                            pl.when(c > 0)(lambda: cross_sum(c - 1))
                    for b in (0, 1):
                        e = 2 * i + b
                        at = pl.ds(pl.multiple_of(e * cap, 16), cap)

                        @pl.when(c == 0)
                        def _():
                            for s in (0, 1):
                                src = 2 * (1 - side) + s
                                cmat[s, at, :] = jnp.where(
                                    slot_rows == slots_of(src, e), gates_of(src, e), 0.0).astype(BF16)
                    for b in (0, 1):
                        e = 2 * i + b
                        at = pl.ds(pl.multiple_of(e * cap, 16), cap)
                        pos = (side * nc + c) * n_e + e
                        slot = pos % DRING
                        dfilled(slot)
                        o = dot(h[e], wdr[slot]).astype(BF16)
                        outs[0, at, :] = o[:cap]
                        outs[1, at, :] = o[cap:]
                        if side == 0:
                            dfill(pos + DRING)
                        else:
                            pl.when(pos < 2 * nc * n_e - DRING)(lambda pos=pos: dfill(pos + DRING))
                    return 0

                lax.fori_loop(0, n_e // 2, body, 0)
                for s in (1, 0):
                    for t in range(0, tokens, 256):
                        y = combined(s, t)
                        if s == 1:
                            (lsend if side else qsend)[c, t : t + 256, :] = y.astype(BF16)
                        elif side:
                            yo[c, t : t + 256, :] = y
                        else:
                            yp[t : t + 256, :] = y
                if side:
                    l_copy(c).start()
                    o_copy(c).start()
                else:
                    q_copy(c).start()
                return 0

            lax.fori_loop(0, nc, chunk, 0)

        down(0, hr)

        def last_sum(i):
            pl.when(i == 0)(lambda: cross_sum(nc - 1))

        near(len(phases) - 1, late, last_sum)
        down(1, hl)
        for c in range(nc):
            q_copy(c).wait_send()
            l_copy(c).wait_send()
            l_copy(c).wait_recv()
            o_copy(c).wait()
        for c in range(nc):
            c_copy(c).wait_send()
            c_copy(c).wait_recv()

    pl.run_scoped(
        second_half,
        pltpu.VMEM((2, n_e * cap, CC), BF16),
        pltpu.VMEM((2, n_e * cap, tokens), BF16),
        pltpu.VMEM((tokens, CC), F32),
        pltpu.VMEM((nc, tokens, CC), BF16),
        pltpu.VMEM((nc, tokens, CC), BF16),
        pltpu.VMEM((nc, tokens, CC), BF16),
        pltpu.VMEM((nc, tokens, CC), F32),
    )
    for src in (1, 2, 3):
        meta_copy(src).wait_send()
        for k in range(nk):
            x_copy(src, k).wait_send()


def moe(meta, x, w_gate, w_up, w_down, cap):
    tokens, d = x.shape
    n_e, _, ff = w_gate.shape
    nk, nc = d // KC, d // CC
    dma = pltpu.SemaphoreType.DMA
    hbm = pl.BlockSpec(memory_space=pl.ANY)
    return pl.pallas_call(
        functools.partial(moe_kernel, cap),
        out_shape=[
            jax.ShapeDtypeStruct((tokens, d), F32),
            jax.ShapeDtypeStruct((tokens, d), BF16),
            jax.ShapeDtypeStruct((tokens, d), BF16),
        ],
        in_specs=[pl.BlockSpec(memory_space=pltpu.VMEM)] + [hbm] * 4,
        out_specs=[hbm] * 3,
        scratch_shapes=[
            pltpu.VMEM((4, *meta.shape), F32),
            pltpu.VMEM((4, nk, tokens, KC), BF16),
            pltpu.VMEM((RING, KC, ff), BF16),
            pltpu.VMEM((RING, KC, ff), BF16),
            pltpu.VMEM((DRING, ff, CC), BF16),
            pltpu.VMEM((n_e, 2 * cap, ff), BF16),
            pltpu.VMEM((n_e, 2 * cap, ff), BF16),
            pltpu.VMEM((nc, tokens, CC), BF16),
            pltpu.VMEM((2, 2 * cap, KC), BF16),
            pltpu.VMEM((2 * cap, d), BF16),
            dma((RING,)), dma((RING,)), dma((DRING,)), dma((nk,)),
            dma((3,)), dma((3,)), dma((3, nk)), dma((3, nk)),
            dma((nc,)), dma((nc,)), dma((nc,)), dma((nc,)), dma((nc,)), dma((nc,)), dma((nc,)),
        ],
        compiler_params=pltpu.CompilerParams(
            collective_id=0, has_side_effects=True, vmem_limit_bytes=67_043_328),
        cost_estimate=pl.CostEstimate(
            flops=24 * n_e * cap * d * ff, bytes_accessed=12 * n_e * d * ff, transcendentals=0),
    )(meta, x, w_gate, w_up, w_down)


def solution(mesh):
    members = mesh.shape["ep"]

    def local(x, expert, slot, gate, w_gate, w_up, w_down):
        x = x[0, 0]
        tokens, _ = x.shape
        top = expert.shape[-1]
        cap = 5 * tokens * top // (4 * w_gate.shape[0] * members)
        meta = jnp.concatenate(
            [expert[0, 0].T.astype(F32), jnp.minimum(slot[0, 0], cap).T.astype(F32),
             gate[0, 0].T.astype(BF16).astype(F32)], axis=0)
        own, near, far = moe(meta, x, w_gate, w_up, w_down, cap)
        y = own + near.astype(F32) + far.astype(F32)
        return y.astype(BF16)[None, None]

    tok = P("dp", "ep", None, None)
    w = P("ep", None, None)
    return jax.shard_map(local, mesh=mesh, in_specs=(tok,) * 4 + (w,) * 3, out_specs=tok, check_vma=False)
```

time: 743 us -> 173 us (0.23)
  matrix products: 252 us -> 0 us
  blocking collectives: 242 us -> 0 us
  waiting for transfers between devices: 219 us -> 0 us
  Pallas kernels: 0 us -> 164 us
  local copies, waits for them, and re-layouts: 19.6 us -> 0 us
  other arithmetic: 0.01 us -> 7.99 us
  starting transfers between devices: 7.87 us -> 0 us
    dot_general x7 -> x0, matrix products: 252 us -> none  [einsum(): return jnp.einsum(form, a.astype(jnp.float32), b.astype(jnp.float32))]
    another operation x1 -> x0, blocking collectives: 242 us -> none  [placed(): return lax.with_sharding_constraint(v, NamedSharding(mesh, P(*spec)))]
    another operation x1 -> x0, waiting for transfers between devices: 219 us -> none  [placed(): return lax.with_sharding_constraint(v, NamedSharding(mesh, P(*spec)))]
    pallas_call x0 -> x1, Pallas kernels: none -> 164 us  [moe(): pl.pallas_call(functools.partial(moe_kernel, cap), out_shape=[jax.ShapeDt...]
    another operation x1 -> x0, local copies, waits for them, and re-layouts: 17.6 us -> none  [placed(): return lax.with_sharding_constraint(v, NamedSharding(mesh, P(*spec)))]
    another operation x1 -> x0, starting transfers between devices: 7.87 us -> none  [placed(): return lax.with_sharding_constraint(v, NamedSharding(mesh, P(*spec)))]
  transfers between devices with their start and end apart: 1 -> 0, of which waited for: 1 -> 0; matrix products, arithmetic and copies ran while one was open for 1% -> 0% of each run, Pallas kernels for 0% -> 0%
where the time goes in v2:
time: 173 us; the launch traced here: 172 us
  Pallas kernels  164 us (95%)
  other arithmetic  7.99 us (5%)
    pallas_call x1, Pallas kernels, moe(): pl.pallas_call(functools.partial(moe_kernel, cap), out_shape=[jax.ShapeDt...  164 us
    broadcast_in_dim x1, other arithmetic, local(): return y.astype(BF16)[None, None]  5.91 us

profile of v2, /device:TPU:0, one launch (start us, length us, event | category | flops | bytes accessed | tf_op | source)
XLA Modules:
  0.0 172.4 jit_solution(4664124112258026648)
XLA Ops:
  0.0 0.7 convert_bitcast_fusion
  0.7 0.7 convert_bitcast_fusion.1
  1.5 0.6 pad_maximum_fusion.meta_ref
  2.1 164.4 %shard_map.73 = (f32[512,2048]{1,0:T(8,128)}, bf16[512,2048]{1,0:T(8,128)(2,1)}, bf16[512,2048]{1,0:T(8,128)(2,1)}) custom-call(f32[24,512]{1,0:T(8,128)} %pad_maximum_fusion.meta_ref, bf16[512,2048]{1,0:T(8,128)(2,1)} %bitcast.16, bf16[16,2048,1024]{2,1,0:T(8,128)(2,1)} %wg_ref.1, bf16[16,2048,1024]{2,1,0:T(8,128)(2,1)} %wu_ref.1, ...), custom_call_target="tpu_custom_call" | custom-call | flops 64424509440 | bytes 402653184 | tf_op jit(solution)/shard_map/pallas_call | solution.py:325
  166.5 5.9 %fusion = bf16[1,1,512,2048]{3,2,1,0:T(8,128)(2,1)} fusion(bf16[512,2048]{1,0:T(8,128)(2,1)} %get-tuple-element.10, f32[512,2048]{1,0:T(8,128)} %get-tuple-element.8, bf16[512,2048]{1,0:T(8,128)(2,1)} %get-tuple-element.9), kind=kLoop, calls=%fused_computation.1 | loop fusion | flops 5242880 | bytes 10485760 | tf_op jit(solution)/shard_map/broadcast_in_dim | solution.py:369

commit v3 on v2

--- a/solution.py
+++ b/solution.py
@@ -10,8 +10,8 @@
 F32, BF16 = jnp.float32, jnp.bfloat16
 MESH = pl.DeviceIdType.MESH
 
-EARLY = 6
-RING, DRING = 8, 4
+EARLY = 7
+RING, DRING = 8, 6
 KC, CC, FB = 512, 512, 256
 
 
@@ -71,7 +71,7 @@
         return pltpu.make_async_copy(x_ref.at[:, pl.ds(k * KC, KC)], xs.at[0, k], xsem.at[k])
 
     def x_copy(src, k):
-        piece_ref = xs.at[2, k] if src == 3 else x_ref.at[:, pl.ds(k * KC, KC)]
+        piece_ref = xs.at[2 if src == 3 else 0, k]
         return pltpu.make_async_remote_copy(
             src_ref=piece_ref, dst_ref=xs.at[src, k], send_sem=xsend.at[src - 1, k],
             recv_sem=xrecv.at[src - 1, k], device_id={"ep": far if src == 2 else sib}, device_id_type=MESH)
@@ -83,16 +83,19 @@
 
     for k in range(nk):
         x_local(k).start()
-    for pos in range(RING):
-        fill(pos, pos // 4, pos % 4)
+    for pos in range(4):
+        fill(pos, 0, pos)
     metas[0] = meta_ref[...]
     pl.semaphore_wait(barrier, 3)
     for src in (1, 2, 3):
         meta_copy(src).start()
     for k in range(nk):
+        x_local(k).wait()
+        if k == 0:
+            x_copy(2, k).start()
         x_copy(1, k).start()
-    for k in range(nk):
-        x_copy(2, k).start()
+    for pos in range(4, RING):
+        fill(pos, 1, pos - 4)
 
     slot_rows = lax.broadcasted_iota(jnp.int32, (cap, tokens), 0).astype(F32)
 
@@ -143,6 +146,10 @@
 
         lax.fori_loop(0, count, body, 0)
 
+    def send_next(k):
+        x_copy(2, k - 1).wait_send()
+        x_copy(2, k).start()
+
     def pass_on(k):
         x_copy(2, k).wait_recv()
         x_copy(3, k).start()
@@ -156,6 +163,10 @@
                 @pl.when(i == n_e // 2 - 1)
                 def _():
                     pass_on(k + 1)
+            if k + 2 < nk:
+                @pl.when(i == 4 + k)
+                def _():
+                    send_next(k + 2)
             for b in (0, 1):
                 for s in (0, 1):
                     zr[b, s * cap : (s + 1) * cap, :] = dot(pick(2 + s, 2 * i + b), xs[2 + s, k]).astype(BF16)
@@ -181,11 +192,14 @@
         lax.fori_loop(0, n_e // 2, body, 0)
 
     for k in range(nk):
-        x_local(k).wait()
         x_copy(1, k).wait_recv()
     meta_copy(1).wait_recv()
 
     def first_pass_on(i):
+        @pl.when(i == EARLY // 2)
+        def _():
+            send_next(1)
+
         @pl.when(i == EARLY - 2)
         def _():
             pass_on(0)
@@ -313,7 +327,8 @@
     for src in (1, 2, 3):
         meta_copy(src).wait_send()
         for k in range(nk):
-            x_copy(src, k).wait_send()
+            if src != 2 or k == nk - 1:
+                x_copy(src, k).wait_send()
 
 
 def moe(meta, x, w_gate, w_up, w_down, cap):

time: 173 us -> 170 us (0.983)
  Pallas kernels: 164 us -> 161 us
    pallas_call x1, Pallas kernels: 164 us -> 161 us  [moe(): pl.pallas_call(functools.partial(moe_kernel, cap), out_shape=[jax.ShapeDt...]
where the time goes in v3:
time: 170 us; the launch traced here: 169 us
  Pallas kernels  161 us (95%)
  other arithmetic  7.99 us (5%)
    pallas_call x1, Pallas kernels, moe(): pl.pallas_call(functools.partial(moe_kernel, cap), out_shape=[jax.ShapeDt...  161 us
    broadcast_in_dim x1, other arithmetic, local(): return y.astype(BF16)[None, None]  5.91 us

profile of v3, /device:TPU:0, one launch (start us, length us, event | category | flops | bytes accessed | tf_op | source)
XLA Modules:
  0.0 169.2 jit_solution(1083767962738891085)
XLA Ops:
  0.0 0.7 convert_bitcast_fusion
  0.7 0.7 convert_bitcast_fusion.1
  1.5 0.6 pad_maximum_fusion.meta_ref
  2.1 161.2 %shard_map.73 = (f32[512,2048]{1,0:T(8,128)}, bf16[512,2048]{1,0:T(8,128)(2,1)}, bf16[512,2048]{1,0:T(8,128)(2,1)}) custom-call(f32[24,512]{1,0:T(8,128)} %pad_maximum_fusion.meta_ref, bf16[512,2048]{1,0:T(8,128)(2,1)} %bitcast.16, bf16[16,2048,1024]{2,1,0:T(8,128)(2,1)} %wg_ref.1, bf16[16,2048,1024]{2,1,0:T(8,128)(2,1)} %wu_ref.1, ...), custom_call_target="tpu_custom_call" | custom-call | flops 64424509440 | bytes 402653184 | tf_op jit(solution)/shard_map/pallas_call | solution.py:340
  163.3 5.9 %fusion = bf16[1,1,512,2048]{3,2,1,0:T(8,128)(2,1)} fusion(bf16[512,2048]{1,0:T(8,128)(2,1)} %get-tuple-element.10, f32[512,2048]{1,0:T(8,128)} %get-tuple-element.8, bf16[512,2048]{1,0:T(8,128)(2,1)} %get-tuple-element.9), kind=kLoop, calls=%fused_computation.1 | loop fusion | flops 5242880 | bytes 10485760 | tf_op jit(solution)/shard_map/broadcast_in_dim | solution.py:384

commit v4 on v2

v4 whole, which is shorter than its diff:
```python
import functools

import jax
import jax.numpy as jnp
from jax import lax
from jax.experimental import pallas as pl
from jax.experimental.pallas import tpu as pltpu
from jax.sharding import PartitionSpec as P

F32, BF16 = jnp.float32, jnp.bfloat16
MESH = pl.DeviceIdType.MESH

RING, DRING = 4, 8
KC, CC, FB = 512, 512, 256


def moe_kernel(cap, meta_ref, x_ref, wg_ref, wu_ref, wd_ref, own_ref, sibr_ref, crossr_ref,
               metas, xs, wgr, wur, hl, zr,
               gsem, usem, dsem, xsem, msend, mrecv, xsend, xrecv,
               qsend_sem, qrecv_sem, csend_sem, crecv_sem, lsend_sem, lrecv_sem, osem, free_sem):
    me = lax.axis_index("ep")
    sib = me + 1 - 2 * (me % 2)
    far = (me + 2) % 4
    peers = (sib, far, (sib + 2) % 4)
    n_e, d, ff = wg_ref.shape
    top, tokens = metas.shape[1] // 3, metas.shape[2]
    nk, nc = d // KC, d // CC
    first = me * n_e
    near_rows, far_rows = slice(0, 2 * cap), slice(2 * cap, 4 * cap)

    barrier = pltpu.get_barrier_semaphore()
    for p in peers:
        pl.semaphore_signal(barrier, inc=1, device_id={"ep": p}, device_id_type=MESH)

    def fill(pos):
        slot, e, k = pos % RING, pos % n_e, pos // n_e
        rows = pl.ds(k * KC if isinstance(k, int) else pl.multiple_of(k * KC, KC), KC)
        pltpu.make_async_copy(wg_ref.at[e, rows], wgr.at[slot], gsem.at[slot]).start()
        pltpu.make_async_copy(wu_ref.at[e, rows], wur.at[slot], usem.at[slot]).start()

    def filled(slot):
        pltpu.make_async_copy(wg_ref.at[0, pl.ds(0, KC)], wgr.at[slot], gsem.at[slot]).wait()
        pltpu.make_async_copy(wu_ref.at[0, pl.ds(0, KC)], wur.at[slot], usem.at[slot]).wait()

    def x_local(k):
        return pltpu.make_async_copy(x_ref.at[:, pl.ds(k * KC, KC)], xs.at[k, 0], xsem.at[k])

    def x_copy(src, k):
        return pltpu.make_async_remote_copy(
            src_ref=xs.at[k, 2 if src == 3 else 0], dst_ref=xs.at[k, src], send_sem=xsend.at[src - 1, k],
            recv_sem=xrecv.at[src - 1, k], device_id={"ep": far if src == 2 else sib}, device_id_type=MESH)

    def meta_copy(src):
        return pltpu.make_async_remote_copy(
            src_ref=meta_ref, dst_ref=metas.at[src], send_sem=msend.at[src - 1],
            recv_sem=mrecv.at[src - 1], device_id={"ep": peers[src - 1]}, device_id_type=MESH)

    for k in range(nk):
        x_local(k).start()
    metas[0] = meta_ref[...]
    pl.semaphore_wait(barrier, 3)
    for src in (1, 2, 3):
        meta_copy(src).start()
    for k in range(nk):
        x_local(k).wait()
        if k == 0:
            x_copy(2, k).start()
        x_copy(1, k).start()
    for pos in range(RING):
        fill(pos)

    slot_rows = lax.broadcasted_iota(jnp.int32, (cap, tokens), 0).astype(F32)

    def slots_of(src, e):
        hit = metas[src, 0:top, :] == (e + first).astype(F32)
        return jnp.max(jnp.where(hit, metas[src, top : 2 * top, :], -1.0), axis=0, keepdims=True)

    def gates_of(src, e):
        hit = metas[src, 0:top, :] == (e + first).astype(F32)
        return jnp.sum(jnp.where(hit, metas[src, 2 * top :, :], 0.0), axis=0, keepdims=True)

    def pick(src, e):
        return jnp.where(slot_rows == slots_of(src, e), 1.0, 0.0).astype(BF16)

    def dot(a, b):
        return jnp.dot(a, b, preferred_element_type=F32)

    def far_hidden(e, half):
        block = 2 * e + half
        slab = block // 3
        return slab // 4, slab % 4, pl.ds(pl.multiple_of((block % 3) * (2 * cap), 16), 2 * cap)

    def send_next(k):
        x_copy(2, k - 1).wait_send()
        x_copy(2, k).start()

    def pass_on(k):
        x_copy(2, k).wait_recv()
        x_copy(3, k).start()

    def up_phase(k, acc):
        x_copy(1, k).wait_recv()
        x_copy(3, k).wait_recv()
        if k == nk - 1:
            for n in range(k):
                x_copy(1, n).wait_send()
                x_copy(3, n).wait_send()

        def body(i, _):
            if k + 2 < nk:
                @pl.when(i == 5)
                def _():
                    send_next(k + 2)
            if k + 1 < nk:
                @pl.when(i == n_e // 2 - 1)
                def _():
                    pass_on(k + 1)
            for src in range(4):
                both = jnp.concatenate([pick(src, 2 * i), pick(src, 2 * i + 1)], axis=0)
                z = dot(both, xs[k, src]).astype(BF16)
                zr[0, src * cap : (src + 1) * cap, :] = z[:cap]
                zr[1, src * cap : (src + 1) * cap, :] = z[cap:]
            for b in (0, 1):
                e = 2 * i + b
                pos = k * n_e + e
                slot = pos % RING
                filled(slot)
                for f in range(0, ff, FB):
                    g = dot(zr[b], wgr[slot, :, f : f + FB])
                    u = dot(zr[b], wur[slot, :, f : f + FB])
                    if k:
                        g = g + acc[e, :, f : f + FB]
                        u = u + acc[e, :, ff + f : ff + f + FB]
                    if k == nk - 1:
                        h = (g * jax.nn.sigmoid(g) * u).astype(BF16)
                        hl[e, :, f : f + FB] = h[near_rows]
                        k2, s2, rows = far_hidden(e, f // KC)
                        xs[k2, s2, rows, f % KC : f % KC + FB] = h[far_rows]
                    else:
                        acc[e, :, f : f + FB] = g
                        acc[e, :, ff + f : ff + f + FB] = u
                if k < nk - 1:
                    fill(pos + RING)
                else:
                    pl.when(e < n_e - RING)(lambda pos=pos: fill(pos + RING))
            return 0

        lax.fori_loop(0, n_e // 2, body, 0)

    for src in (1, 2, 3):
        meta_copy(src).wait_recv()
    send_next(1)
    pass_on(0)

    def first_half(acc):
        for k in range(nk):
            up_phase(k, acc)

    pl.run_scoped(first_half, pltpu.VMEM((n_e, 4 * cap, 2 * ff), F32))

    for src in (1, 2, 3):
        meta_copy(src).wait_send()
        x_copy(src, nk - 1).wait_send()
    pl.semaphore_signal(free_sem, inc=1, device_id={"ep": sib}, device_id_type=MESH)

    def second_half(wdr, outs, cmat, yp, qsend, csend, lsend, yo):
        def cols(c):
            return pl.ds(c * CC if isinstance(c, int) else pl.multiple_of(c * CC, CC), CC)

        def dfill(pos):
            slot, e, c = pos % DRING, pos % n_e, pos // n_e
            pltpu.make_async_copy(wd_ref.at[e, :, cols(c)], wdr.at[slot], dsem.at[slot]).start()

        def dfilled(slot):
            pltpu.make_async_copy(wd_ref.at[0, :, pl.ds(0, CC)], wdr.at[slot], dsem.at[slot]).wait()

        def q_copy(c):
            return pltpu.make_async_remote_copy(
                src_ref=qsend.at[c], dst_ref=xs.at[nk - 1, c], send_sem=qsend_sem.at[c],
                recv_sem=qrecv_sem.at[c], device_id={"ep": sib}, device_id_type=MESH)

        def c_copy(c):
            return pltpu.make_async_remote_copy(
                src_ref=csend.at[c], dst_ref=crossr_ref.at[:, cols(c)], send_sem=csend_sem.at[c],
                recv_sem=crecv_sem.at[c], device_id={"ep": far}, device_id_type=MESH)

        def l_copy(c):
            return pltpu.make_async_remote_copy(
                src_ref=lsend.at[c], dst_ref=sibr_ref.at[:, cols(c)], send_sem=lsend_sem.at[c],
                recv_sem=lrecv_sem.at[c], device_id={"ep": sib}, device_id_type=MESH)

        def o_copy(c):
            return pltpu.make_async_copy(yo.at[c], own_ref.at[:, cols(c)], osem.at[c])

        for pos in range(DRING):
            dfill(pos)

        def cross_sum(c):
            q_copy(c).wait_recv()
            csend[c] = (yp[...] + xs[nk - 1, c].astype(F32)).astype(BF16)
            c_copy(c).start()

        def weigh(src, e):
            at = pl.ds(pl.multiple_of(e * cap, 16), cap)
            cmat[src, at, :] = jnp.where(slot_rows == slots_of(src, e), gates_of(src, e), 0.0).astype(BF16)

        def combined(src, t):
            return lax.dot_general(cmat[src, :, t : t + 256], outs[src], (((0,), (0,)), ((), ())),
                                   preferred_element_type=F32)

        def chunk(c, _):
            def body(i, _):
                @pl.when(i == 3)
                def _():
                    pl.when(c > 0)(lambda: cross_sum(c - 1))

                @pl.when(c == 0)
                def _():
                    for b in (0, 1):
                        weigh(2, 2 * i + b)
                        weigh(3, 2 * i + b)

                for b in (0, 1):
                    e = 2 * i + b
                    at = pl.ds(pl.multiple_of(e * cap, 16), cap)
                    pos = c * n_e + e
                    slot = pos % DRING
                    dfilled(slot)
                    o = dot(hl[e], wdr[slot]).astype(BF16)
                    outs[0, at, :] = o[:cap]
                    outs[1, at, :] = o[cap:]
                    o = None
                    for half in range(ff // KC):
                        k2, s2, rows = far_hidden(e, half)
                        p = dot(xs[k2, s2, rows, :], wdr[slot, half * KC : (half + 1) * KC, :])
                        o = p if o is None else o + p
                    o = o.astype(BF16)
                    outs[2, at, :] = o[:cap]
                    outs[3, at, :] = o[cap:]
                    pl.when(pos < nc * n_e - DRING)(lambda pos=pos: dfill(pos + DRING))
                return 0

            lax.fori_loop(0, n_e // 2, body, 0)
            for t in range(0, tokens, 256):
                qsend[c, t : t + 256, :] = combined(3, t).astype(BF16)
            for t in range(0, tokens, 256):
                yp[t : t + 256, :] = combined(2, t)
            pl.when(c == 0)(lambda: pl.semaphore_wait(free_sem, 1))
            q_copy(c).start()

            @pl.when(c == 0)
            def _():
                def near_weights(e, _):
                    weigh(0, e)
                    weigh(1, e)
                    return 0

                lax.fori_loop(0, n_e, near_weights, 0)

            for t in range(0, tokens, 256):
                lsend[c, t : t + 256, :] = combined(1, t).astype(BF16)
            for t in range(0, tokens, 256):
                yo[c, t : t + 256, :] = combined(0, t)
            l_copy(c).start()
            o_copy(c).start()
            return 0

        lax.fori_loop(0, nc, chunk, 0)
        cross_sum(nc - 1)
        for c in range(nc):
            q_copy(c).wait_send()
            l_copy(c).wait_send()
            l_copy(c).wait_recv()
            o_copy(c).wait()
        for c in range(nc):
            c_copy(c).wait_send()
            c_copy(c).wait_recv()

    pl.run_scoped(
        second_half,
        pltpu.VMEM((DRING, ff, CC), BF16),
        pltpu.VMEM((4, n_e * cap, CC), BF16),
        pltpu.VMEM((4, n_e * cap, tokens), BF16),
        pltpu.VMEM((tokens, CC), F32),
        pltpu.VMEM((nc, tokens, CC), BF16),
        pltpu.VMEM((nc, tokens, CC), BF16),
        pltpu.VMEM((nc, tokens, CC), BF16),
        pltpu.VMEM((nc, tokens, CC), F32),
    )


def moe(meta, x, w_gate, w_up, w_down, cap):
    tokens, d = x.shape
    n_e, _, ff = w_gate.shape
    nk, nc = d // KC, d // CC
    dma = pltpu.SemaphoreType.DMA
    hbm = pl.BlockSpec(memory_space=pl.ANY)
    return pl.pallas_call(
        functools.partial(moe_kernel, cap),
        out_shape=[
            jax.ShapeDtypeStruct((tokens, d), F32),
            jax.ShapeDtypeStruct((tokens, d), BF16),
            jax.ShapeDtypeStruct((tokens, d), BF16),
        ],
        in_specs=[pl.BlockSpec(memory_space=pltpu.VMEM)] + [hbm] * 4,
        out_specs=[hbm] * 3,
        scratch_shapes=[
            pltpu.VMEM((4, *meta.shape), F32),
            pltpu.VMEM((nk, 4, tokens, KC), BF16),
            pltpu.VMEM((RING, KC, ff), BF16),
            pltpu.VMEM((RING, KC, ff), BF16),
            pltpu.VMEM((n_e, 2 * cap, ff), BF16),
            pltpu.VMEM((2, 4 * cap, KC), BF16),
            dma((RING,)), dma((RING,)), dma((DRING,)), dma((nk,)),
            dma((3,)), dma((3,)), dma((3, nk)), dma((3, nk)),
            dma((nc,)), dma((nc,)), dma((nc,)), dma((nc,)), dma((nc,)), dma((nc,)), dma((nc,)),
            pltpu.SemaphoreType.REGULAR,
        ],
        compiler_params=pltpu.CompilerParams(
            collective_id=0, has_side_effects=True, vmem_limit_bytes=67_043_328),
        cost_estimate=pl.CostEstimate(
            flops=24 * n_e * cap * d * ff, bytes_accessed=6 * n_e * d * ff, transcendentals=0),
    )(meta, x, w_gate, w_up, w_down)


def solution(mesh):
    members = mesh.shape["ep"]

    def local(x, expert, slot, gate, w_gate, w_up, w_down):
        x = x[0, 0]
        tokens, _ = x.shape
        top = expert.shape[-1]
        cap = 5 * tokens * top // (4 * w_gate.shape[0] * members)
        meta = jnp.concatenate(
            [expert[0, 0].T.astype(F32), jnp.minimum(slot[0, 0], cap).T.astype(F32),
             gate[0, 0].T.astype(BF16).astype(F32)], axis=0)
        own, near, far = moe(meta, x, w_gate, w_up, w_down, cap)
        y = own + near.astype(F32) + far.astype(F32)
        return y.astype(BF16)[None, None]

    tok = P("dp", "ep", None, None)
    w = P("ep", None, None)
    return jax.shard_map(local, mesh=mesh, in_specs=(tok,) * 4 + (w,) * 3, out_specs=tok, check_vma=False)
```

time: 173 us -> 169 us (0.977)
  Pallas kernels: 164 us -> 161 us
    pallas_call x1, Pallas kernels: 164 us -> 161 us  [moe(): pl.pallas_call(functools.partial(moe_kernel, cap), out_shape=[jax.ShapeDt...]
where the time goes in v4:
time: 169 us
  Pallas kernels  161 us (95%)
  other arithmetic  7.99 us (5%)
    pallas_call x1, Pallas kernels, moe(): pl.pallas_call(functools.partial(moe_kernel, cap), out_shape=[jax.ShapeDt...  161 us
    broadcast_in_dim x1, other arithmetic, local(): return y.astype(BF16)[None, None]  5.91 us

profile of v4, /device:TPU:0, one launch (start us, length us, event | category | flops | bytes accessed | tf_op | source)
XLA Modules:
  0.0 169.1 jit_solution(6729242348996112961)
XLA Ops:
  0.0 0.7 convert_bitcast_fusion
  0.7 0.7 convert_bitcast_fusion.1
  1.5 0.6 pad_maximum_fusion.meta_ref
  2.1 161.1 %shard_map.73 = (f32[512,2048]{1,0:T(8,128)}, bf16[512,2048]{1,0:T(8,128)(2,1)}, bf16[512,2048]{1,0:T(8,128)(2,1)}) custom-call(f32[24,512]{1,0:T(8,128)} %pad_maximum_fusion.meta_ref, bf16[512,2048]{1,0:T(8,128)(2,1)} %bitcast.16, bf16[16,2048,1024]{2,1,0:T(8,128)(2,1)} %wg_ref.1, bf16[16,2048,1024]{2,1,0:T(8,128)(2,1)} %wu_ref.1, ...), custom_call_target="tpu_custom_call" | custom-call | flops 64424509440 | bytes 201326592 | tf_op jit(solution)/shard_map/pallas_call | solution.py:298
  163.2 5.9 %fusion = bf16[1,1,512,2048]{3,2,1,0:T(8,128)(2,1)} fusion(bf16[512,2048]{1,0:T(8,128)(2,1)} %get-tuple-element.10, f32[512,2048]{1,0:T(8,128)} %get-tuple-element.8, bf16[512,2048]{1,0:T(8,128)(2,1)} %get-tuple-element.9), kind=kLoop, calls=%fused_computation.1 | loop fusion | flops 5242880 | bytes 10485760 | tf_op jit(solution)/shard_map/broadcast_in_dim | solution.py:339

commit v5 on v4

--- a/solution.py
+++ b/solution.py
@@ -108,20 +108,20 @@
 
         def body(i, _):
             if k + 2 < nk:
-                @pl.when(i == 5)
+                @pl.when(i == 2)
                 def _():
                     send_next(k + 2)
             if k + 1 < nk:
-                @pl.when(i == n_e // 2 - 1)
+                @pl.when(i == n_e // 4 - 1)
                 def _():
                     pass_on(k + 1)
             for src in range(4):
-                both = jnp.concatenate([pick(src, 2 * i), pick(src, 2 * i + 1)], axis=0)
-                z = dot(both, xs[k, src]).astype(BF16)
-                zr[0, src * cap : (src + 1) * cap, :] = z[:cap]
-                zr[1, src * cap : (src + 1) * cap, :] = z[cap:]
-            for b in (0, 1):
-                e = 2 * i + b
+                four = jnp.concatenate([pick(src, 4 * i + b) for b in range(4)], axis=0)
+                z = dot(four, xs[k, src]).astype(BF16)
+                for b in range(4):
+                    zr[b, src * cap : (src + 1) * cap, :] = z[b * cap : (b + 1) * cap]
+            for b in range(4):
+                e = 4 * i + b
                 pos = k * n_e + e
                 slot = pos % RING
                 filled(slot)
@@ -145,7 +145,7 @@
                     pl.when(e < n_e - RING)(lambda pos=pos: fill(pos + RING))
             return 0
 
-        lax.fori_loop(0, n_e // 2, body, 0)
+        lax.fori_loop(0, n_e // 4, body, 0)
 
     for src in (1, 2, 3):
         meta_copy(src).wait_recv()
@@ -181,12 +181,12 @@
 
         def c_copy(c):
             return pltpu.make_async_remote_copy(
-                src_ref=csend.at[c], dst_ref=crossr_ref.at[:, cols(c)], send_sem=csend_sem.at[c],
+                src_ref=csend.at[c], dst_ref=crossr_ref.at[c], send_sem=csend_sem.at[c],
                 recv_sem=crecv_sem.at[c], device_id={"ep": far}, device_id_type=MESH)
 
         def l_copy(c):
             return pltpu.make_async_remote_copy(
-                src_ref=lsend.at[c], dst_ref=sibr_ref.at[:, cols(c)], send_sem=lsend_sem.at[c],
+                src_ref=lsend.at[c], dst_ref=sibr_ref.at[c], send_sem=lsend_sem.at[c],
                 recv_sem=lrecv_sem.at[c], device_id={"ep": sib}, device_id_type=MESH)
 
         def o_copy(c):
@@ -226,17 +226,16 @@
                     pos = c * n_e + e
                     slot = pos % DRING
                     dfilled(slot)
-                    o = dot(hl[e], wdr[slot]).astype(BF16)
-                    outs[0, at, :] = o[:cap]
-                    outs[1, at, :] = o[cap:]
                     o = None
                     for half in range(ff // KC):
                         k2, s2, rows = far_hidden(e, half)
-                        p = dot(xs[k2, s2, rows, :], wdr[slot, half * KC : (half + 1) * KC, :])
+                        part = slice(half * KC, (half + 1) * KC)
+                        h = jnp.concatenate([hl[e, :, part], xs[k2, s2, rows, :]], axis=0)
+                        p = dot(h, wdr[slot, part, :])
                         o = p if o is None else o + p
                     o = o.astype(BF16)
-                    outs[2, at, :] = o[:cap]
-                    outs[3, at, :] = o[cap:]
+                    for src in range(4):
+                        outs[src, at, :] = o[src * cap : (src + 1) * cap]
                     pl.when(pos < nc * n_e - DRING)(lambda pos=pos: dfill(pos + DRING))
                 return 0
 
@@ -299,8 +298,8 @@
         functools.partial(moe_kernel, cap),
         out_shape=[
             jax.ShapeDtypeStruct((tokens, d), F32),
-            jax.ShapeDtypeStruct((tokens, d), BF16),
-            jax.ShapeDtypeStruct((tokens, d), BF16),
+            jax.ShapeDtypeStruct((nc, tokens, CC), BF16),
+            jax.ShapeDtypeStruct((nc, tokens, CC), BF16),
         ],
         in_specs=[pl.BlockSpec(memory_space=pltpu.VMEM)] + [hbm] * 4,
         out_specs=[hbm] * 3,
@@ -310,7 +309,7 @@
             pltpu.VMEM((RING, KC, ff), BF16),
             pltpu.VMEM((RING, KC, ff), BF16),
             pltpu.VMEM((n_e, 2 * cap, ff), BF16),
-            pltpu.VMEM((2, 4 * cap, KC), BF16),
+            pltpu.VMEM((4, 4 * cap, KC), BF16),
             dma((RING,)), dma((RING,)), dma((DRING,)), dma((nk,)),
             dma((3,)), dma((3,)), dma((3, nk)), dma((3, nk)),
             dma((nc,)), dma((nc,)), dma((nc,)), dma((nc,)), dma((nc,)), dma((nc,)), dma((nc,)),
@@ -323,6 +322,25 @@
     )(meta, x, w_gate, w_up, w_down)
 
 
+def total_kernel(own_ref, near_ref, far_ref, y_ref):
+    y_ref[...] = (own_ref[...] + near_ref[0].astype(F32) + far_ref[0].astype(F32)).astype(BF16)
+
+
+def total(own, near, far):
+    tokens, d = own.shape
+    rows = tokens // 2
+    flat = pl.BlockSpec((rows, CC), lambda c, r: (r, c))
+    piece = pl.BlockSpec((1, rows, CC), lambda c, r: (c, r, 0))
+    return pl.pallas_call(
+        total_kernel,
+        grid=(d // CC, 2),
+        out_shape=jax.ShapeDtypeStruct((tokens, d), BF16),
+        in_specs=[flat, piece, piece],
+        out_specs=flat,
+        cost_estimate=pl.CostEstimate(flops=2 * tokens * d, bytes_accessed=10 * tokens * d, transcendentals=0),
+    )(own, near, far)
+
+
 def solution(mesh):
     members = mesh.shape["ep"]
 
@@ -335,8 +353,8 @@
             [expert[0, 0].T.astype(F32), jnp.minimum(slot[0, 0], cap).T.astype(F32),
              gate[0, 0].T.astype(BF16).astype(F32)], axis=0)
         own, near, far = moe(meta, x, w_gate, w_up, w_down, cap)
-        y = own + near.astype(F32) + far.astype(F32)
-        return y.astype(BF16)[None, None]
+        y = total(own, near, far)
+        return y[None, None]
 
     tok = P("dp", "ep", None, None)
     w = P("ep", None, None)

time: 169 us -> 166 us (0.982)
  other arithmetic: 7.99 us -> 2.08 us
  Pallas kernels: 161 us -> 163 us
    pallas_call x0 -> x1, Pallas kernels: none -> 7.03 us  [total(): pl.pallas_call(total_kernel, grid=(d // CC, 2), out_shape=jax.ShapeDtypeS...]
    broadcast_in_dim x1 -> x0, other arithmetic: 5.91 us -> none  [local(): return y.astype(BF16)[None, None]]
    pallas_call x1, Pallas kernels: 161 us -> 156 us  [moe(): pl.pallas_call(functools.partial(moe_kernel, cap), out_shape=[jax.ShapeDt...]
where the time goes in v5:
time: 166 us
  Pallas kernels  163 us (98%)
  other arithmetic  2.08 us (1%)
    pallas_call x1, Pallas kernels, moe(): pl.pallas_call(functools.partial(moe_kernel, cap), out_shape=[jax.ShapeDt...  156 us
    pallas_call x1, Pallas kernels, total(): pl.pallas_call(total_kernel, grid=(d // CC, 2), out_shape=jax.ShapeDtypeS...  7.03 us

profile of v5, /device:TPU:0, one launch (start us, length us, event | category | flops | bytes accessed | tf_op | source)
XLA Modules:
  0.0 165.6 jit_solution(7234729054648543519)
XLA Ops:
  0.0 0.7 convert_bitcast_fusion
  0.7 0.7 convert_bitcast_fusion.1
  1.5 0.6 pad_maximum_fusion.meta_ref
  2.1 156.4 %shard_map.73 = (f32[512,2048]{1,0:T(8,128)}, bf16[4,512,512]{2,1,0:T(8,128)(2,1)}, bf16[4,512,512]{2,1,0:T(8,128)(2,1)}) custom-call(f32[24,512]{1,0:T(8,128)} %pad_maximum_fusion.meta_ref, bf16[512,2048]{1,0:T(8,128)(2,1)} %bitcast.15, bf16[16,2048,1024]{2,1,0:T(8,128)(2,1)} %wg_ref.1, bf16[16,2048,1024]{2,1,0:T(8,128)(2,1)} %wu_ref.1, ...), custom_call_target="tpu_custom_call" | custom-call | flops 64424509440 | bytes 201326592 | tf_op jit(solution)/shard_map/pallas_call | solution.py:297
  158.5 7.0 %shard_map.74 = bf16[512,2048]{1,0:T(8,128)(2,1)} custom-call(f32[512,2048]{1,0:T(8,128)} %get-tuple-element.8.own_ref, bf16[4,512,512]{2,1,0:T(8,128)(2,1)} %get-tuple-element.9.near_ref, bf16[4,512,512]{2,1,0:T(8,128)(2,1)} %get-tuple-element.10.far_ref), custom_call_target="tpu_custom_call" | custom-call | flops 2097152 | bytes 10485760 | tf_op jit(solution)/shard_map/pallas_call | solution.py:334
